TPU v7x, 32 devices: a whole 2x2x4 slice. The times are simulated.
32 devices in a mesh: band: 4 (over y, x), grid: 8 (over z, core).
Axes of the slice: x: 2, y: 2, z: 4, core: 2. Of those that a mesh axis runs over, the one named last changes fastest.
Arguments:
- wavefunctions: bfloat16 [1024, 131072], P('band', 'grid'), may hold values from -6 to 6
- projectors: bfloat16 [512, 8, 13, 256], P('grid'), may hold values from -0.0068359375 to 0.0068359375
- slot_atom: int32 [512, 8], P('grid'), may hold values from -1 to 255, as said below
- occupations: float32 [1024], P('band'), may hold values from 0.02 to 2
Outputs:
- density: float32 [256, 13, 13], P('grid')
Inputs may be any that keep to these rules, and one draw needn't show every extreme that they name: `slot_atom`: -1 marks an empty slot. Any other entry is an atom a whose owning domain a // 32 lies within 3 domains, counted around the closed cycle of 8 domains, of the domain of the block, block index // 64. In every domain some block has all 8 slots filled.
All inputs are finite; a program needn't handle non-finite values.
Results may differ from a plain program's by a relative error of at most 0.0003.
Values sent between devices are 32-bit elements; how exact they have to be, the bound alone decides.
A program may use at most 64 MiB of HBM per device.

v0:
```python
import jax
import jax.numpy as jnp
from jax import lax
from jax.sharding import PartitionSpec as P

REACH = 3
ATOMS_DEV = 32


def shifted(block, axis, distance):
    devices = range(lax.axis_size(axis))
    route = [((i - distance) % len(devices), i) for i in devices]
    return lax.ppermute(block, axis, route)


def body(wavefunctions, projectors, slot_atom, occupations):
    band_count = wavefunctions.shape[0]
    block_count, capacity, proj_count, block_len = projectors.shape
    domains = lax.axis_size("grid")
    domain = lax.axis_index("grid")
    window_len = 2 * REACH + 1
    row_len = proj_count * band_count
    grid_blocks = wavefunctions.reshape(band_count, block_count, block_len)
    stacked = projectors.reshape(block_count, capacity * proj_count, block_len)
    slot_terms = jnp.einsum(
        "ngb,gcb->gcn", grid_blocks, stacked, preferred_element_type=jnp.float32
    )
    slot_terms = slot_terms.reshape(block_count * capacity, row_len)
    slot_ids = slot_atom.reshape(-1)
    owner = jnp.floor_divide(slot_ids, ATOMS_DEV)
    offset = jnp.mod(owner - domain + REACH, domains)
    target = jnp.where(
        slot_ids >= 0, offset * ATOMS_DEV + jnp.mod(slot_ids, ATOMS_DEV), window_len * ATOMS_DEV
    )
    selector = (
        jnp.arange(window_len * ATOMS_DEV, dtype=jnp.int32)[:, None] == target[None, :]
    ).astype(jnp.float32)
    window = jnp.dot(
        selector, slot_terms, precision=lax.Precision.HIGHEST, preferred_element_type=jnp.float32
    )
    window = window.reshape(window_len, ATOMS_DEV, row_len)
    forward = window[2 * REACH]
    for hop in range(REACH, 0, -1):
        forward = shifted(forward, "grid", 1) + window[REACH + hop - 1]
    backward = window[0]
    for hop in range(REACH, 0, -1):
        addend = window[REACH - hop + 1] if hop > 1 else jnp.zeros_like(backward)
        backward = shifted(backward, "grid", -1) + addend
    owned = forward + backward
    owned = owned.reshape(ATOMS_DEV, proj_count, band_count)
    weighted = owned * occupations.reshape(1, 1, band_count)
    partial_sum = jnp.einsum("ain,ajn->aij", weighted, owned, precision=lax.Precision.HIGHEST)
    density = lax.psum(partial_sum, "band")
    return density


def solution(mesh):
    in_specs = (P("band", "grid"), P("grid", None, None, None), P("grid", None), P("band"))
    out_specs = P("grid", None, None)
    return jax.shard_map(body, mesh=mesh, in_specs=in_specs, out_specs=out_specs, check_vma=False)
```

profile of v0, /device:TPU:0, one launch (start us, length us, event | category | flops | bytes accessed | tf_op | source)
XLA Modules:
  0.0 87.4 jit_solution(6354588679132287062)
XLA Ops:
  0.0 2.8 %copy.8 = bf16[64,8,13,256]{3,0,2,1:T(8,128)(2,1)S(1)} copy(bf16[64,8,13,256]{3,1,2,0:T(8,128)(2,1)} %param.5) | data formatting | bytes 6815744 | tf_op args[1]
  2.8 9.4 %fusion = f32[64,104,256]{2,1,0:T(8,128)} fusion(bf16[32,64,8,256]{3,2,1,0:T(8,128)(2,1)} %bitcast.8, bf16[64,104,256]{2,0,1:T(8,128)(2,1)S(1)} %bitcast.7), kind=kOutput, calls=%fused_computation | convolution fusion | flops 872415232 | bytes 18612224 | tf_op jit(solution)/shard_map/ngb,gcb->gcn/dot_general | solution.py:25
  12.2 0.0 copy-start
  12.2 8.5 %reshape.103 = f32[512,3328]{1,0:T(8,128)} reshape(f32[64,104,256]{2,1,0:T(8,128)} %fusion) | data formatting | bytes 13631488 | tf_op jit(solution)/shard_map/reshape | solution.py:28
  20.7 0.0 copy-done
  20.7 0.1 copy.7
  20.7 0.1 reshape.100
  20.9 6.3 %fusion.6 = f32[224,3328]{1,0:T(8,128)S(1)} fusion(f32[512,3328]{1,0:T(8,128)} %reshape.103, s32[512]{0:T(512)S(1)} %fusion.15), kind=kOutput, calls=%fused_computation.7 | convolution fusion | flops 4580294656 | bytes 9799680 | tf_op jit(solution)/shard_map/dot_general | solution.py:38
  27.1 0.1 fusion.17
  27.2 0.5 collective-permute-start
  27.8 0.0 copy-start.1
  27.8 4.1 %collective-permute-start.3 = (f32[32,3328]{1,0:T(8,128)S(1)}, f32[32,3328]{1,0:T(8,128)S(1)}, u32[]{:S(2)}, u32[]{:S(2)}) collective-permute-start(f32[32,3328]{1,0:T(8,128)S(1)} %get-tuple-element.10), channel_id=1, source_target_pairs={{1,0},{2,1},{3,2},{4,3},{5,4},{6,5},{7,6},{0,7},{9,8},{10,9},{11,1... | collective-permute-start | bytes 1277960 | tf_op jit(solution)/shard_map/ppermute | solution.py:13
  31.9 7.7 %collective-permute-done = f32[32,3328]{1,0:T(8,128)S(1)} collective-permute-done((f32[32,3328]{1,0:T(8,128)S(1)}, f32[32,3328]{1,0:T(8,128)S(1)}, u32[]{:S(2)}, u32[]{:S(2)}) %collective-permute-start) | collective-permute-done | bytes 426016 | tf_op jit(solution)/shard_map/ppermute | solution.py:13
  39.6 0.4 collective-permute-done.3
  40.0 0.1 slice_add_fusion.4
  40.1 2.0 %collective-permute-start.1 = (f32[32,3328]{1,0:T(8,128)S(1)}, f32[32,3328]{1,0:T(8,128)S(1)}, u32[]{:S(2)}, u32[]{:S(2)}) collective-permute-start(f32[32,3328]{1,0:T(8,128)S(1)} %get-tuple-element.7), channel_id=1, source_target_pairs={{7,0},{0,1},{1,2},{2,3},{3,4},{4,5},{5,6},{6,7},{15,8},{8,9},{9,10... | collective-permute-start | bytes 1277960 | tf_op jit(solution)/shard_map/ppermute | solution.py:13
  42.1 1.8 %collective-permute-start.4 = (f32[32,3328]{1,0:T(8,128)S(1)}, f32[32,3328]{1,0:T(8,128)S(1)}, u32[]{:S(2)}, u32[]{:S(2)}) collective-permute-start(f32[32,3328]{1,0:T(8,128)S(1)} %get-tuple-element.8), channel_id=1, source_target_pairs={{1,0},{2,1},{3,2},{4,3},{5,4},{6,5},{7,6},{0,7},{9,8},{10,9},{11,1... | collective-permute-start | bytes 1277960 | tf_op jit(solution)/shard_map/ppermute | solution.py:13
  44.0 7.6 %collective-permute-done.1 = f32[32,3328]{1,0:T(8,128)S(1)} collective-permute-done((f32[32,3328]{1,0:T(8,128)S(1)}, f32[32,3328]{1,0:T(8,128)S(1)}, u32[]{:S(2)}, u32[]{:S(2)}) %collective-permute-start.1) | collective-permute-done | bytes 426016 | tf_op jit(solution)/shard_map/ppermute | solution.py:13
  51.5 0.2 collective-permute-done.4
  51.7 0.1 slice_add_fusion.3
  51.8 2.5 %collective-permute-start.2 = (f32[32,3328]{1,0:T(8,128)S(1)}, f32[32,3328]{1,0:T(8,128)S(1)}, u32[]{:S(2)}, u32[]{:S(2)}) collective-permute-start(f32[32,3328]{1,0:T(8,128)S(1)} %get-tuple-element.5), channel_id=1, source_target_pairs={{7,0},{0,1},{1,2},{2,3},{3,4},{4,5},{5,6},{6,7},{15,8},{8,9},{9,10... | collective-permute-start | bytes 1277960 | tf_op jit(solution)/shard_map/ppermute | solution.py:13
  54.2 1.4 %collective-permute-start.5 = (f32[32,3328]{1,0:T(8,128)S(1)}, f32[32,3328]{1,0:T(8,128)S(1)}, u32[]{:S(2)}, u32[]{:S(2)}) collective-permute-start(f32[32,3328]{1,0:T(8,128)S(1)} %get-tuple-element.6), channel_id=1, source_target_pairs={{1,0},{2,1},{3,2},{4,3},{5,4},{6,5},{7,6},{0,7},{9,8},{10,9},{11,1... | collective-permute-start | bytes 1277960 | tf_op jit(solution)/shard_map/ppermute | solution.py:13
  55.7 7.1 %collective-permute-done.2 = f32[32,3328]{1,0:T(8,128)S(1)} collective-permute-done((f32[32,3328]{1,0:T(8,128)S(1)}, f32[32,3328]{1,0:T(8,128)S(1)}, u32[]{:S(2)}, u32[]{:S(2)}) %collective-permute-start.2) | collective-permute-done | bytes 426016 | tf_op jit(solution)/shard_map/ppermute | solution.py:13
  62.8 1.0 %collective-permute-done.5 = f32[32,3328]{1,0:T(8,128)S(1)} collective-permute-done((f32[32,3328]{1,0:T(8,128)S(1)}, f32[32,3328]{1,0:T(8,128)S(1)}, u32[]{:S(2)}, u32[]{:S(2)}) %collective-permute-start.5) | collective-permute-done | bytes 426016 | tf_op jit(solution)/shard_map/ppermute | solution.py:13
  63.8 0.1 fusion.7
  63.9 0.1 reshape.104
  64.0 0.0 copy-done.1
  64.0 0.6 fusion.4
  64.7 21.9 %psum.7 = f32[32,13,13]{2,1,0:T(8,128)S(1)} all-reduce(f32[32,13,13]{2,1,0:T(8,128)S(1)} %fusion.4), channel_id=1, replica_groups=mesh['band'=4,'grid'=8] {'band'}, use_global_device_ids=true, to_apply=%region_0.1 | all-reduce | flops 5408 | bytes 43264 | tf_op jit(solution)/shard_map/psum | solution.py:53
  86.6 0.8 copy.11
  (1 shorter events, 0.0 us)
Async XLA Ops:
  12.2 8.5 %copy-start = (s32[64,8]{0,1:T(8,128)S(1)}, s32[64,8]{0,1:T(8,128)}, u32[]{:S(2)}) copy-start(s32[64,8]{0,1:T(8,128)} %param.6) | copy-start | bytes 6148
  27.2 12.3 %collective-permute-start = (f32[32,3328]{1,0:T(8,128)S(1)}, f32[32,3328]{1,0:T(8,128)S(1)}, u32[]{:S(2)}, u32[]{:S(2)}) collective-permute-start(f32[32,3328]{1,0:T(8,128)S(1)} %get-tuple-element.9), channel_id=1, source_target_pairs={{7,0},{0,1},{1,2},{2,3},{3,4},{4,5},{5,6},{6,7},{15,8},{8,9},{9,10... | collective-permute-start | bytes 1277960 | tf_op jit(solution)/shard_map/ppermute | solution.py:13
  27.8 36.3 %copy-start.1 = (f32[256]{0:T(256)S(1)}, f32[256]{0:T(256)}, u32[]{:S(2)}) copy-start(f32[256]{0:T(256)} %param.7) | copy-start | bytes 3076
  27.8 12.2 %collective-permute-start.3 = (f32[32,3328]{1,0:T(8,128)S(1)}, f32[32,3328]{1,0:T(8,128)S(1)}, u32[]{:S(2)}, u32[]{:S(2)}) collective-permute-start(f32[32,3328]{1,0:T(8,128)S(1)} %get-tuple-element.10), channel_id=1, source_target_pairs={{1,0},{2,1},{3,2},{4,3},{5,4},{6,5},{7,6},{0,7},{9,8},{10,9},{11,1... | collective-permute-start | bytes 1277960 | tf_op jit(solution)/shard_map/ppermute | solution.py:13
  40.1 11.5 %collective-permute-start.1 = (f32[32,3328]{1,0:T(8,128)S(1)}, f32[32,3328]{1,0:T(8,128)S(1)}, u32[]{:S(2)}, u32[]{:S(2)}) collective-permute-start(f32[32,3328]{1,0:T(8,128)S(1)} %get-tuple-element.7), channel_id=1, source_target_pairs={{7,0},{0,1},{1,2},{2,3},{3,4},{4,5},{5,6},{6,7},{15,8},{8,9},{9,10... | collective-permute-start | bytes 1277960 | tf_op jit(solution)/shard_map/ppermute | solution.py:13
  42.1 9.6 %collective-permute-start.4 = (f32[32,3328]{1,0:T(8,128)S(1)}, f32[32,3328]{1,0:T(8,128)S(1)}, u32[]{:S(2)}, u32[]{:S(2)}) collective-permute-start(f32[32,3328]{1,0:T(8,128)S(1)} %get-tuple-element.8), channel_id=1, source_target_pairs={{1,0},{2,1},{3,2},{4,3},{5,4},{6,5},{7,6},{0,7},{9,8},{10,9},{11,1... | collective-permute-start | bytes 1277960 | tf_op jit(solution)/shard_map/ppermute | solution.py:13
  51.8 11.0 %collective-permute-start.2 = (f32[32,3328]{1,0:T(8,128)S(1)}, f32[32,3328]{1,0:T(8,128)S(1)}, u32[]{:S(2)}, u32[]{:S(2)}) collective-permute-start(f32[32,3328]{1,0:T(8,128)S(1)} %get-tuple-element.5), channel_id=1, source_target_pairs={{7,0},{0,1},{1,2},{2,3},{3,4},{4,5},{5,6},{6,7},{15,8},{8,9},{9,10... | collective-permute-start | bytes 1277960 | tf_op jit(solution)/shard_map/ppermute | solution.py:13
  54.2 9.6 %collective-permute-start.5 = (f32[32,3328]{1,0:T(8,128)S(1)}, f32[32,3328]{1,0:T(8,128)S(1)}, u32[]{:S(2)}, u32[]{:S(2)}) collective-permute-start(f32[32,3328]{1,0:T(8,128)S(1)} %get-tuple-element.6), channel_id=1, source_target_pairs={{1,0},{2,1},{3,2},{4,3},{5,4},{6,5},{7,6},{0,7},{9,8},{10,9},{11,1... | collective-permute-start | bytes 1277960 | tf_op jit(solution)/shard_map/ppermute | solution.py:13
where the time goes:
time: 87.8 us; the launch traced here: 87.4 us
  waiting for transfers between devices  24 us (27%)
  blocking collectives  21.9 us (25%)
  matrix products  16.3 us (19%)
  local copies, waits for them, and re-layouts  12.4 us (14%)
  starting transfers between devices  12.4 us (14%)
    ppermute x6, waiting for transfers between devices, shifted(): return lax.ppermute(block, axis, route)  24 us
    psum x1, blocking collectives, body(): density = lax.psum(partial_sum, 'band')  21.9 us
    ppermute x6, starting transfers between devices, shifted(): return lax.ppermute(block, axis, route)  12.4 us
    dot_general x1, matrix products, body(): jnp.einsum('ngb,gcb->gcn', grid_blocks, stacked, preferred_element_type=j...  9.38 us
    reshape x1, local copies, waits for them, and re-layouts, body(): slot_terms = slot_terms.reshape(block_count * capacity, row_len)  8.49 us
    dot_general x1, matrix products, body(): jnp.dot(selector, slot_terms, precision=lax.Precision.HIGHEST, preferred_...  6.29 us
    unnamed x6, local copies, waits for them, and re-layouts  2.86 us
  transfers between devices with their start and end apart: 6, of which 6 were waited for; matrix products, arithmetic and copies ran while one was open for 0% of the time, Pallas kernels for 0%

commit v1 on v0

--- a/solution.py
+++ b/solution.py
@@ -50,7 +50,9 @@
     owned = owned.reshape(ATOMS_DEV, proj_count, band_count)
     weighted = owned * occupations.reshape(1, 1, band_count)
     partial_sum = jnp.einsum("ain,ajn->aij", weighted, owned, precision=lax.Precision.HIGHEST)
-    density = lax.psum(partial_sum, "band")
+    density = partial_sum
+    for hop_ in (1, 2):
+        density = density + lax.ppermute(density, "band", [(dev, dev ^ hop_) for dev in range(4)])
     return density
 
 

time: 87.8 us -> 83 us (0.945)
  blocking collectives: 21.9 us -> 0 us
  waiting for transfers between devices: 24 us -> 37.1 us
  starting transfers between devices: 12.4 us -> 16.3 us
    psum x1 -> x0, blocking collectives: 21.9 us -> none  [body(): density = lax.psum(partial_sum, 'band')]
    ppermute x0 -> x2, waiting for transfers between devices: none -> 13.1 us  [body(): lax.ppermute(density, 'band', [(dev, dev ^ hop_) for dev in range(4)])]
    ppermute x0 -> x2, starting transfers between devices: none -> 3.91 us  [body(): lax.ppermute(density, 'band', [(dev, dev ^ hop_) for dev in range(4)])]
  transfers between devices with their start and end apart: 6 -> 8, of which waited for: 6 -> 8; matrix products, arithmetic and copies ran while one was open for 0% -> 0% of each run, Pallas kernels for 0% -> 0%
where the time goes in v1:
time: 83 us; the launch traced here: 82.6 us
  waiting for transfers between devices  37.1 us (45%)
  matrix products  16.3 us (20%)
  starting transfers between devices  16.3 us (20%)
  local copies, waits for them, and re-layouts  12.5 us (15%)
    ppermute x6, waiting for transfers between devices, shifted(): return lax.ppermute(block, axis, route)  24 us
    ppermute x2, waiting for transfers between devices, body(): lax.ppermute(density, 'band', [(dev, dev ^ hop_) for dev in range(4)])  13.1 us
    ppermute x6, starting transfers between devices, shifted(): return lax.ppermute(block, axis, route)  12.4 us
    dot_general x1, matrix products, body(): jnp.einsum('ngb,gcb->gcn', grid_blocks, stacked, preferred_element_type=j...  9.42 us
    reshape x1, local copies, waits for them, and re-layouts, body(): slot_terms = slot_terms.reshape(block_count * capacity, row_len)  8.49 us
    dot_general x1, matrix products, body(): jnp.dot(selector, slot_terms, precision=lax.Precision.HIGHEST, preferred_...  6.29 us
    ppermute x2, starting transfers between devices, body(): lax.ppermute(density, 'band', [(dev, dev ^ hop_) for dev in range(4)])  3.91 us
    unnamed x6, local copies, waits for them, and re-layouts  2.86 us
  transfers between devices with their start and end apart: 8, of which 8 were waited for; matrix products, arithmetic and copies ran while one was open for 0% of the time, Pallas kernels for 0%

profile of v1, /device:TPU:0, one launch (start us, length us, event | category | flops | bytes accessed | tf_op | source)
XLA Modules:
  0.0 82.6 jit_solution(6742691558252321003)
XLA Ops:
  0.0 2.8 %copy.8 = bf16[64,8,13,256]{3,0,2,1:T(8,128)(2,1)S(1)} copy(bf16[64,8,13,256]{3,1,2,0:T(8,128)(2,1)} %param.5) | data formatting | bytes 6815744 | tf_op args[1]
  2.8 9.4 %fusion = f32[64,104,256]{2,1,0:T(8,128)} fusion(bf16[32,64,8,256]{3,2,1,0:T(8,128)(2,1)} %bitcast.8, bf16[64,104,256]{2,0,1:T(8,128)(2,1)S(1)} %bitcast.7), kind=kOutput, calls=%fused_computation | convolution fusion | flops 872415232 | bytes 18612224 | tf_op jit(solution)/shard_map/ngb,gcb->gcn/dot_general | solution.py:25
  12.2 0.0 copy-start
  12.2 8.5 %reshape.103 = f32[512,3328]{1,0:T(8,128)} reshape(f32[64,104,256]{2,1,0:T(8,128)} %fusion) | data formatting | bytes 13631488 | tf_op jit(solution)/shard_map/reshape | solution.py:28
  20.7 0.0 copy-done
  20.7 0.1 copy.7
  20.8 0.1 reshape.100
  20.9 6.3 %fusion.6 = f32[224,3328]{1,0:T(8,128)S(1)} fusion(f32[512,3328]{1,0:T(8,128)} %reshape.103, s32[512]{0:T(512)S(1)} %fusion.15), kind=kOutput, calls=%fused_computation.7 | convolution fusion | flops 4580294656 | bytes 9799680 | tf_op jit(solution)/shard_map/dot_general | solution.py:38
  27.2 0.1 fusion.17
  27.3 0.5 collective-permute-start
  27.8 0.0 copy-start.1
  27.8 4.1 %collective-permute-start.3 = (f32[32,3328]{1,0:T(8,128)S(1)}, f32[32,3328]{1,0:T(8,128)S(1)}, u32[]{:S(2)}, u32[]{:S(2)}) collective-permute-start(f32[32,3328]{1,0:T(8,128)S(1)} %get-tuple-element.10), channel_id=1, source_target_pairs={{1,0},{2,1},{3,2},{4,3},{5,4},{6,5},{7,6},{0,7},{9,8},{10,9},{11,1... | collective-permute-start | bytes 1277960 | tf_op jit(solution)/shard_map/ppermute | solution.py:13
  31.9 7.7 %collective-permute-done = f32[32,3328]{1,0:T(8,128)S(1)} collective-permute-done((f32[32,3328]{1,0:T(8,128)S(1)}, f32[32,3328]{1,0:T(8,128)S(1)}, u32[]{:S(2)}, u32[]{:S(2)}) %collective-permute-start) | collective-permute-done | bytes 426016 | tf_op jit(solution)/shard_map/ppermute | solution.py:13
  39.6 0.4 collective-permute-done.3
  40.0 0.1 slice_add_fusion.4
  40.1 2.0 %collective-permute-start.1 = (f32[32,3328]{1,0:T(8,128)S(1)}, f32[32,3328]{1,0:T(8,128)S(1)}, u32[]{:S(2)}, u32[]{:S(2)}) collective-permute-start(f32[32,3328]{1,0:T(8,128)S(1)} %get-tuple-element.7), channel_id=1, source_target_pairs={{7,0},{0,1},{1,2},{2,3},{3,4},{4,5},{5,6},{6,7},{15,8},{8,9},{9,10... | collective-permute-start | bytes 1277960 | tf_op jit(solution)/shard_map/ppermute | solution.py:13
  42.2 1.8 %collective-permute-start.4 = (f32[32,3328]{1,0:T(8,128)S(1)}, f32[32,3328]{1,0:T(8,128)S(1)}, u32[]{:S(2)}, u32[]{:S(2)}) collective-permute-start(f32[32,3328]{1,0:T(8,128)S(1)} %get-tuple-element.8), channel_id=1, source_target_pairs={{1,0},{2,1},{3,2},{4,3},{5,4},{6,5},{7,6},{0,7},{9,8},{10,9},{11,1... | collective-permute-start | bytes 1277960 | tf_op jit(solution)/shard_map/ppermute | solution.py:13
  44.0 7.6 %collective-permute-done.1 = f32[32,3328]{1,0:T(8,128)S(1)} collective-permute-done((f32[32,3328]{1,0:T(8,128)S(1)}, f32[32,3328]{1,0:T(8,128)S(1)}, u32[]{:S(2)}, u32[]{:S(2)}) %collective-permute-start.1) | collective-permute-done | bytes 426016 | tf_op jit(solution)/shard_map/ppermute | solution.py:13
  51.6 0.2 collective-permute-done.4
  51.8 0.1 slice_add_fusion.3
  51.8 2.5 %collective-permute-start.2 = (f32[32,3328]{1,0:T(8,128)S(1)}, f32[32,3328]{1,0:T(8,128)S(1)}, u32[]{:S(2)}, u32[]{:S(2)}) collective-permute-start(f32[32,3328]{1,0:T(8,128)S(1)} %get-tuple-element.5), channel_id=1, source_target_pairs={{7,0},{0,1},{1,2},{2,3},{3,4},{4,5},{5,6},{6,7},{15,8},{8,9},{9,10... | collective-permute-start | bytes 1277960 | tf_op jit(solution)/shard_map/ppermute | solution.py:13
  54.3 1.4 %collective-permute-start.5 = (f32[32,3328]{1,0:T(8,128)S(1)}, f32[32,3328]{1,0:T(8,128)S(1)}, u32[]{:S(2)}, u32[]{:S(2)}) collective-permute-start(f32[32,3328]{1,0:T(8,128)S(1)} %get-tuple-element.6), channel_id=1, source_target_pairs={{1,0},{2,1},{3,2},{4,3},{5,4},{6,5},{7,6},{0,7},{9,8},{10,9},{11,1... | collective-permute-start | bytes 1277960 | tf_op jit(solution)/shard_map/ppermute | solution.py:13
  55.7 7.1 %collective-permute-done.2 = f32[32,3328]{1,0:T(8,128)S(1)} collective-permute-done((f32[32,3328]{1,0:T(8,128)S(1)}, f32[32,3328]{1,0:T(8,128)S(1)}, u32[]{:S(2)}, u32[]{:S(2)}) %collective-permute-start.2) | collective-permute-done | bytes 426016 | tf_op jit(solution)/shard_map/ppermute | solution.py:13
  62.9 1.0 %collective-permute-done.5 = f32[32,3328]{1,0:T(8,128)S(1)} collective-permute-done((f32[32,3328]{1,0:T(8,128)S(1)}, f32[32,3328]{1,0:T(8,128)S(1)}, u32[]{:S(2)}, u32[]{:S(2)}) %collective-permute-start.5) | collective-permute-done | bytes 426016 | tf_op jit(solution)/shard_map/ppermute | solution.py:13
  63.9 0.1 fusion.7
  63.9 0.1 reshape.104
  64.1 0.0 copy-done.1
  64.1 0.6 fusion.4
  64.7 1.9 %collective-permute-start.6 = (f32[32,13,13]{2,1,0:T(8,128)S(1)}, f32[32,13,13]{2,1,0:T(8,128)S(1)}, u32[]{:S(2)}, u32[]{:S(2)}) collective-permute-start(f32[32,13,13]{2,1,0:T(8,128)S(1)} %fusion.4), channel_id=1, source_target_pairs={{0,8},{8,0},{16,24},{24,16},{1,9},{9,1},{17,25},{25,17},{2,10},{10... | collective-permute-start | bytes 64904 | tf_op jit(solution)/shard_map/ppermute | solution.py:55
  66.6 6.1 %collective-permute-done.6 = f32[32,13,13]{2,1,0:T(8,128)S(1)} collective-permute-done((f32[32,13,13]{2,1,0:T(8,128)S(1)}, f32[32,13,13]{2,1,0:T(8,128)S(1)}, u32[]{:S(2)}, u32[]{:S(2)}) %collective-permute-start.6) | collective-permute-done | bytes 21664 | tf_op jit(solution)/shard_map/ppermute | solution.py:55
  72.7 2.0 %collective-permute-start.7 = (f32[32,13,13]{2,1,0:T(8,128)S(1)}, f32[32,13,13]{2,1,0:T(8,128)S(1)}, u32[]{:S(2)}, u32[]{:S(2)}) collective-permute-start(f32[32,13,13]{2,1,0:T(8,128)S(1)} %add.75), channel_id=1, source_target_pairs={{0,16},{8,24},{16,0},{24,8},{1,17},{9,25},{17,1},{25,9},{2,18},{10... | collective-permute-start | bytes 64904 | tf_op jit(solution)/shard_map/ppermute | solution.py:55
  74.7 7.0 %collective-permute-done.7 = f32[32,13,13]{2,1,0:T(8,128)S(1)} collective-permute-done((f32[32,13,13]{2,1,0:T(8,128)S(1)}, f32[32,13,13]{2,1,0:T(8,128)S(1)}, u32[]{:S(2)}, u32[]{:S(2)}) %collective-permute-start.7) | collective-permute-done | bytes 21664 | tf_op jit(solution)/shard_map/ppermute | solution.py:55
  81.8 0.8 copy.11
  (3 shorter events, 0.1 us)
Async XLA Ops:
  12.2 8.5 %copy-start = (s32[64,8]{0,1:T(8,128)S(1)}, s32[64,8]{0,1:T(8,128)}, u32[]{:S(2)}) copy-start(s32[64,8]{0,1:T(8,128)} %param.6) | copy-start | bytes 6148
  27.3 12.3 %collective-permute-start = (f32[32,3328]{1,0:T(8,128)S(1)}, f32[32,3328]{1,0:T(8,128)S(1)}, u32[]{:S(2)}, u32[]{:S(2)}) collective-permute-start(f32[32,3328]{1,0:T(8,128)S(1)} %get-tuple-element.9), channel_id=1, source_target_pairs={{7,0},{0,1},{1,2},{2,3},{3,4},{4,5},{5,6},{6,7},{15,8},{8,9},{9,10... | collective-permute-start | bytes 1277960 | tf_op jit(solution)/shard_map/ppermute | solution.py:13
  27.8 36.3 %copy-start.1 = (f32[256]{0:T(256)S(1)}, f32[256]{0:T(256)}, u32[]{:S(2)}) copy-start(f32[256]{0:T(256)} %param.7) | copy-start | bytes 3076
  27.8 12.2 %collective-permute-start.3 = (f32[32,3328]{1,0:T(8,128)S(1)}, f32[32,3328]{1,0:T(8,128)S(1)}, u32[]{:S(2)}, u32[]{:S(2)}) collective-permute-start(f32[32,3328]{1,0:T(8,128)S(1)} %get-tuple-element.10), channel_id=1, source_target_pairs={{1,0},{2,1},{3,2},{4,3},{5,4},{6,5},{7,6},{0,7},{9,8},{10,9},{11,1... | collective-permute-start | bytes 1277960 | tf_op jit(solution)/shard_map/ppermute | solution.py:13
  40.1 11.5 %collective-permute-start.1 = (f32[32,3328]{1,0:T(8,128)S(1)}, f32[32,3328]{1,0:T(8,128)S(1)}, u32[]{:S(2)}, u32[]{:S(2)}) collective-permute-start(f32[32,3328]{1,0:T(8,128)S(1)} %get-tuple-element.7), channel_id=1, source_target_pairs={{7,0},{0,1},{1,2},{2,3},{3,4},{4,5},{5,6},{6,7},{15,8},{8,9},{9,10... | collective-permute-start | bytes 1277960 | tf_op jit(solution)/shard_map/ppermute | solution.py:13
  42.2 9.6 %collective-permute-start.4 = (f32[32,3328]{1,0:T(8,128)S(1)}, f32[32,3328]{1,0:T(8,128)S(1)}, u32[]{:S(2)}, u32[]{:S(2)}) collective-permute-start(f32[32,3328]{1,0:T(8,128)S(1)} %get-tuple-element.8), channel_id=1, source_target_pairs={{1,0},{2,1},{3,2},{4,3},{5,4},{6,5},{7,6},{0,7},{9,8},{10,9},{11,1... | collective-permute-start | bytes 1277960 | tf_op jit(solution)/shard_map/ppermute | solution.py:13
  51.8 11.0 %collective-permute-start.2 = (f32[32,3328]{1,0:T(8,128)S(1)}, f32[32,3328]{1,0:T(8,128)S(1)}, u32[]{:S(2)}, u32[]{:S(2)}) collective-permute-start(f32[32,3328]{1,0:T(8,128)S(1)} %get-tuple-element.5), channel_id=1, source_target_pairs={{7,0},{0,1},{1,2},{2,3},{3,4},{4,5},{5,6},{6,7},{15,8},{8,9},{9,10... | collective-permute-start | bytes 1277960 | tf_op jit(solution)/shard_map/ppermute | solution.py:13
  54.3 9.6 %collective-permute-start.5 = (f32[32,3328]{1,0:T(8,128)S(1)}, f32[32,3328]{1,0:T(8,128)S(1)}, u32[]{:S(2)}, u32[]{:S(2)}) collective-permute-start(f32[32,3328]{1,0:T(8,128)S(1)} %get-tuple-element.6), channel_id=1, source_target_pairs={{1,0},{2,1},{3,2},{4,3},{5,4},{6,5},{7,6},{0,7},{9,8},{10,9},{11,1... | collective-permute-start | bytes 1277960 | tf_op jit(solution)/shard_map/ppermute | solution.py:13
  64.7 8.0 %collective-permute-start.6 = (f32[32,13,13]{2,1,0:T(8,128)S(1)}, f32[32,13,13]{2,1,0:T(8,128)S(1)}, u32[]{:S(2)}, u32[]{:S(2)}) collective-permute-start(f32[32,13,13]{2,1,0:T(8,128)S(1)} %fusion.4), channel_id=1, source_target_pairs={{0,8},{8,0},{16,24},{24,16},{1,9},{9,1},{17,25},{25,17},{2,10},{10... | collective-permute-start | bytes 64904 | tf_op jit(solution)/shard_map/ppermute | solution.py:55
  72.7 9.0 %collective-permute-start.7 = (f32[32,13,13]{2,1,0:T(8,128)S(1)}, f32[32,13,13]{2,1,0:T(8,128)S(1)}, u32[]{:S(2)}, u32[]{:S(2)}) collective-permute-start(f32[32,13,13]{2,1,0:T(8,128)S(1)} %add.75), channel_id=1, source_target_pairs={{0,16},{8,24},{16,0},{24,8},{1,17},{9,25},{17,1},{25,9},{2,18},{10... | collective-permute-start | bytes 64904 | tf_op jit(solution)/shard_map/ppermute | solution.py:55
